TPU v7x, 32 devices: a whole 2x2x4 slice. The times are simulated.
32 devices in a mesh: outer: 2 (over x), dp: 16 (over z, y, core).
Axes of the slice: x: 2, y: 2, z: 4, core: 2. Of those that a mesh axis runs over, the one named last changes fastest.
Arguments:
- fast_weights: float32 [2, 4096, 2048], P('outer', 'dp'), may hold values from -6 to 6
- slow_weights: float32 [4096, 2048], P('dp', 'outer'), may hold values from -6 to 6
- momentum: float32 [4096, 2048], P('dp', 'outer'), may hold values from -3 to 3
- tokens: bfloat16 [24576, 4096], P(('outer', 'dp')), may hold values from -6 to 6
- norm_gain: float32 [4096], replicated, may hold values from 0.1 to 1.9
Outputs:
- slow_next: float32 [4096, 2048], P('dp', 'outer')
- momentum_next: float32 [4096, 2048], P('dp', 'outer')
- fast_next: float32 [4096, 2048], P('dp')
- key_values: bfloat16 [24576, 2048], P(('outer', 'dp'))
All inputs are finite; a program needn't handle non-finite values.
Results may differ from a plain program's by a relative error of at most 0.0057.
Values may be sent and summed in bfloat16 or wider, within the bound.
No kernel may reach another device: no remote copies, remote signals or barrier semaphores. Data moves between devices by JAX's collectives and lax.ppermute only.
A program may use at most 128 MiB of HBM per device.

v0:
```python
import jax
import jax.numpy as jnp
from jax import lax
from jax.sharding import PartitionSpec as P

OUTER_LR = 0.7
MOMENTUM_COEF = 0.9
EPSILON = 1e-05


def outer_update(slow_part, moment_part, fast_total, pod_count):
    outer_grad = slow_part - fast_total / pod_count
    moment_next = MOMENTUM_COEF * moment_part + outer_grad
    slow_next = slow_part - OUTER_LR * (outer_grad + MOMENTUM_COEF * moment_next)
    return (slow_next, moment_next)


def body(fast_weights, slow_weights, momentum, tokens, norm_gain):
    pod_count = lax.axis_size("outer")
    width = tokens.shape[1]
    fast_total = lax.psum_scatter(fast_weights[0], "outer", scatter_dimension=1, tiled=True)
    slow_next, momentum_next = outer_update(slow_weights, momentum, fast_total, pod_count)
    fast_next = lax.all_gather(slow_next, "outer", axis=1, tiled=True)
    values = tokens.astype(jnp.float32)
    meansq = jnp.mean(values * values, axis=-1, keepdims=True)
    normed = (values * lax.rsqrt(meansq + EPSILON) * norm_gain).astype(jnp.bfloat16)
    whole_weights = lax.all_gather(fast_next.astype(jnp.bfloat16), "dp", axis=0, tiled=True)
    product = jnp.dot(normed, whole_weights, preferred_element_type=jnp.float32)
    key_values = (product * width ** (-0.5)).astype(jnp.bfloat16)
    return (slow_next, momentum_next, fast_next, key_values)


def solution(mesh):
    in_specs = (
        P("outer", "dp", None),
        P("dp", "outer"),
        P("dp", "outer"),
        P(("outer", "dp"), None),
        P(),
    )
    out_specs = (P("dp", "outer"), P("dp", "outer"), P("dp", None), P(("outer", "dp"), None))
    return jax.shard_map(body, mesh=mesh, in_specs=in_specs, out_specs=out_specs, check_vma=False)
```

profile of v0, /device:TPU:0, one launch (start us, length us, event | category | flops | bytes accessed | tf_op | source)
XLA Modules:
  0.0 238.8 jit_solution(7820645311359404585)
XLA Ops:
  7.2 0.0 reduce-scatter.2.cloned.1.call-start
  7.2 0.7 reduce-scatter.2.cloned.1.call-update
  7.9 0.0 all-gather.3.cloned.1.call-start
  7.9 36.9 %reduce-scatter.2.cloned.1.call-done = f32[256,1024]{1,0:T(8,128)} async-done(((f32[256,2048]{1,0:T(8,128)}), f32[256,1024]{1,0:T(8,128)}) %reduce-scatter.2.cloned.1.call-update) | async-done | bytes 1048592 | tf_op jit(solution)/shard_map/reduce_scatter | solution.py:21
  44.9 3.7 %multiply_subtract_fusion = (f32[256,1024]{1,0:T(8,128)}, f32[256,1024]{1,0:T(8,128)}) fusion(f32[256,1024]{1,0:T(8,128)} %param.6, f32[256,1024]{1,0:T(8,128)} %reduce-scatter.2.cloned.1.call-done, f32[256,1024]{1,0:T(8,128)} %param.7), kind=kLoop, calls=%fused_computation.9 | loop fusion | flops 2097152 | bytes 5242880 | tf_op jit(solution)/shard_map/sub | solution.py:14
  48.6 0.0 copy-start.1
  48.6 0.0 all-gather.3.cloned.1.call-update
  48.6 0.0 all-gather.5.cloned.1.call-start
  48.7 33.2 %all-gather.3.cloned.1.call-done = f32[256,2048]{1,0:T(8,128)} async-done(((f32[256,1024]{1,0:T(8,128)}), f32[256,2048]{1,0:T(8,128)}) %all-gather.3.cloned.1.call-update) | async-done | bytes 2097168 | tf_op jit(solution)/shard_map/all_gather | solution.py:23
  81.9 2.7 %convert_element_type.14 = bf16[256,2048]{1,0:T(8,128)(2,1)} convert(f32[256,2048]{1,0:T(8,128)} %all-gather.3.cloned.1.call-done) | non-fusion elementwise | flops 524288 | bytes 3145728 | tf_op jit(solution)/shard_map/convert_element_type | solution.py:27
  84.6 0.0 all-gather.5.cloned.1.call-update
  84.6 4.1 %fusion = f32[768]{0:T(1024)S(1)} fusion(bf16[768,4096]{1,0:T(8,128)(2,1)} %param.8), kind=kLoop, calls=%fused_computation.2 | loop fusion | flops 9436416 | bytes 6294528 | tf_op jit(solution)/shard_map/reduce_sum | solution.py:25
  88.7 0.0 copy-start
  88.7 122.5 %all-gather.5.cloned.1.call-done = bf16[4096,2048]{1,0:T(8,128)(2,1)} async-done(((bf16[256,2048]{1,0:T(8,128)(2,1)}), bf16[4096,2048]{1,0:T(8,128)(2,1)}) %all-gather.5.cloned.1.call-update) | async-done | bytes 16777232 | tf_op jit(solution)/shard_map/all_gather | solution.py:27
  211.2 0.0 copy-done.1
  211.2 19.7 %multiply_convert_fusion = bf16[768,2048]{1,0:T(8,128)(2,1)} fusion(bf16[4096,2048]{1,0:T(8,128)(2,1)} %all-gather.5.cloned.1.call-done, bf16[768,4096]{1,0:T(8,128)(2,1)} %param.8, f32[4096]{0:T(1024)S(1)} %copy-done.1, f32[768]{0:T(1024)S(1)} %add_rsqrt_fusion), kind=kOutput, calls=%fused_computation.6 | convolution fusion | flops 12900630528 | bytes 26233856 | tf_op jit(solution)/shard_map/dot_general | solution.py:28
  231.0 0.0 copy-done
  231.0 1.3 copy.10
  (1 shorter events, 0.0 us)
Async XLA Ops:
  7.2 37.7 %reduce-scatter.2.cloned.1.call-start = ((), (), s32[]{:S(2)}) async-start(), calls=%async_computation.1 | async-start | bytes 3145728 | tf_op jit(solution)/shard_map/reduce_scatter | solution.py:21
  7.9 74.0 %all-gather.3.cloned.1.call-start = ((), (), s32[]{:S(2)}) async-start(), calls=%async_computation.2 | async-start | bytes 3145728 | tf_op jit(solution)/shard_map/all_gather | solution.py:23
  48.6 162.6 %copy-start.1 = (f32[4096]{0:T(1024)S(1)}, f32[4096]{0:T(1024)}, u32[]{:S(2)}) copy-start(f32[4096]{0:T(1024)} %param.9) | copy-start | bytes 49156
  48.6 162.6 %all-gather.5.cloned.1.call-start = ((), (), s32[]{:S(2)}) async-start(), calls=%async_computation.3 | async-start | bytes 17825792 | tf_op jit(solution)/shard_map/all_gather | solution.py:27
  88.7 142.3 %copy-start = (f32[256,2048]{1,0:T(8,128)S(1)}, f32[256,2048]{1,0:T(8,128)}, u32[]{:S(2)}) copy-start(f32[256,2048]{1,0:T(8,128)} %all-gather.3.cloned.1.call-done) | copy-start | bytes 6291460
Sparse Core Ops, SparseCore 0:
  10.2 34.6 reduce-scatter.1
  48.7 33.0 all-gather.2
  84.7 126.4 all-gather.4
where the time goes:
time: 239 us
  waiting for transfers between devices  193 us (81%)
  matrix products  19.7 us (8%)
  between operations  13.8 us (6%)
  other arithmetic  10.5 us (4%)
    all_gather x1, waiting for transfers between devices, body(): lax.all_gather(fast_next.astype(jnp.bfloat16), 'dp', axis=0, tiled=True)  122 us
    reduce_scatter x1, waiting for transfers between devices, body(): lax.psum_scatter(fast_weights[0], 'outer', scatter_dimension=1, tiled=True)  36.9 us
    all_gather x1, waiting for transfers between devices, body(): fast_next = lax.all_gather(slow_next, 'outer', axis=1, tiled=True)  33.2 us
    dot_general x1, matrix products, body(): product = jnp.dot(normed, whole_weights, preferred_element_type=jnp.float32)  19.7 us
  transfers between devices with their start and end apart: 3, of which 3 were waited for; matrix products, arithmetic and copies ran while one was open for 2% of the time, Pallas kernels for 0%

commit v1 on v0

--- a/solution.py
+++ b/solution.py
@@ -24,7 +24,25 @@
     values = tokens.astype(jnp.float32)
     meansq = jnp.mean(values * values, axis=-1, keepdims=True)
     normed = (values * lax.rsqrt(meansq + EPSILON) * norm_gain).astype(jnp.bfloat16)
-    whole_weights = lax.all_gather(fast_next.astype(jnp.bfloat16), "dp", axis=0, tiled=True)
+    value = fast_next.astype(jnp.bfloat16)
+    size, index, span = (lax.axis_size("dp"), lax.axis_index("dp"), value.shape[0])
+    right = [(i, (i + 1) % size) for i in range(size)]
+    downward = [(i, (i - 1) % size) for i in range(size)]
+    filled = jnp.zeros((*value.shape[:0], size * span, *value.shape[0 + 1 :]), value.dtype)
+    filled = lax.dynamic_update_slice_in_dim(filled, value, index * span, axis=0)
+    from_left = from_right = value
+    half = size // 2
+    for hop in range(1, half + 1):
+        from_left = lax.ppermute(from_left, "dp", right)
+        filled = lax.dynamic_update_slice_in_dim(
+            filled, from_left, (index - hop) % size * span, axis=0
+        )
+        if hop < size - half:
+            from_right = lax.ppermute(from_right, "dp", downward)
+            filled = lax.dynamic_update_slice_in_dim(
+                filled, from_right, (index + hop) % size * span, axis=0
+            )
+    whole_weights = filled
     product = jnp.dot(normed, whole_weights, preferred_element_type=jnp.float32)
     key_values = (product * width ** (-0.5)).astype(jnp.bfloat16)
     return (slow_next, momentum_next, fast_next, key_values)

time: 239 us -> 309 us (1.29)
  the two profiles are of different devices: /device:TPU:0 before, /device:TPU:1 now
where the time goes in v1:
time: 309 us; the launch traced here: 308 us
  waiting for transfers between devices  211 us (68%)
  local copies, waits for them, and re-layouts  38.2 us (12%)
  matrix products  19.7 us (6%)
  starting transfers between devices  19.4 us (6%)
  between operations  14.1 us (5%)
  other arithmetic  6.27 us (2%)
    ppermute x8, waiting for transfers between devices, body(): from_left = lax.ppermute(from_left, 'dp', right)  85.4 us
    ppermute x7, waiting for transfers between devices, body(): from_right = lax.ppermute(from_right, 'dp', downward)  55.1 us
    reduce_scatter x1, waiting for transfers between devices, body(): lax.psum_scatter(fast_weights[0], 'outer', scatter_dimension=1, tiled=True)  36.1 us
    all_gather x1, waiting for transfers between devices, body(): fast_next = lax.all_gather(slow_next, 'outer', axis=1, tiled=True)  33.2 us
    dot_general x1, matrix products, body(): product = jnp.dot(normed, whole_weights, preferred_element_type=jnp.float32)  19.7 us
    ppermute x8, starting transfers between devices, body(): from_left = lax.ppermute(from_left, 'dp', right)  19.3 us
    dynamic_update_slice x8, local copies, waits for them, and re-layouts, body(): lax.dynamic_update_slice_in_dim(filled, from_left, (index - hop) % size *...  14.9 us
    dynamic_update_slice x7, local copies, waits for them, and re-layouts, body(): lax.dynamic_update_slice_in_dim(filled, from_right, (index + hop) % size...  13.9 us
  transfers between devices with their start and end apart: 17, of which 16 were waited for; matrix products, arithmetic and copies ran while one was open for 9% of the time, Pallas kernels for 0%

profile of v1, /device:TPU:1, one launch (start us, length us, event | category | flops | bytes accessed | tf_op | source)
XLA Modules:
  0.0 308.3 jit_solution(7799758165588863300)
XLA Ops:
  7.2 0.0 reduce-scatter.2.cloned.1.call-start
  7.2 0.7 reduce-scatter.2.cloned.1.call-update
  7.9 0.0 all-gather.2.cloned.1.call-start
  7.9 36.1 %reduce-scatter.2.cloned.1.call-done = f32[256,1024]{1,0:T(8,128)} async-done(((f32[256,2048]{1,0:T(8,128)}), f32[256,1024]{1,0:T(8,128)}) %reduce-scatter.2.cloned.1.call-update) | async-done | bytes 1048592 | tf_op jit(solution)/shard_map/reduce_scatter | solution.py:21
  44.1 3.7 %multiply_subtract_fusion = (f32[256,1024]{1,0:T(8,128)}, f32[256,1024]{1,0:T(8,128)}) fusion(f32[256,1024]{1,0:T(8,128)} %param.6, f32[256,1024]{1,0:T(8,128)} %reduce-scatter.2.cloned.1.call-done, f32[256,1024]{1,0:T(8,128)} %param.7), kind=kLoop, calls=%fused_computation.9 | loop fusion | flops 2097152 | bytes 5242880 | tf_op jit(solution)/shard_map/sub | solution.py:14
  47.8 33.2 %all-gather.2.cloned.1.call-done = f32[256,2048]{1,0:T(8,128)} async-done(((f32[256,1024]{1,0:T(8,128)}), f32[256,2048]{1,0:T(8,128)}) %all-gather.2.cloned.1.call-update) | async-done | bytes 2097168 | tf_op jit(solution)/shard_map/all_gather | solution.py:23
  81.1 8.1 %broadcast_in_dim.2 = bf16[4096,2048]{1,0:T(8,128)(2,1)} broadcast(bf16[]{:T(256)} %constant.104.clone.1), dimensions={} | broadcast | bytes 16777218 | tf_op jit(solution)/shard_map/broadcast_in_dim | solution.py:31
  89.1 1.2 constant_dynamic-update-slice_fusion.15
  90.4 1.9 collective-permute-start
  92.3 23.0 %collective-permute-done = bf16[256,2048]{1,0:T(8,128)(2,1)S(1)} collective-permute-done((bf16[256,2048]{1,0:T(8,128)(2,1)S(1)}, bf16[256,2048]{1,0:T(8,128)(2,1)S(1)}, u32[]{:S(2)}, u32[]{:S(2)}) %collective-permute-start) | collective-permute-done | bytes 1048608 | tf_op jit(solution)/shard_map/ppermute | solution.py:36
  115.3 2.5 collective-permute-start.2
  117.8 11.2 %collective-permute-done.1 = bf16[256,2048]{1,0:T(8,128)(2,1)S(1)} collective-permute-done((bf16[256,2048]{1,0:T(8,128)(2,1)S(1)}, bf16[256,2048]{1,0:T(8,128)(2,1)S(1)}, u32[]{:S(2)}, u32[]{:S(2)}) %collective-permute-start.1) | collective-permute-done | bytes 1048608 | tf_op jit(solution)/shard_map/ppermute | solution.py:41
  129.0 10.9 %collective-permute-done.2 = bf16[256,2048]{1,0:T(8,128)(2,1)S(1)} collective-permute-done((bf16[256,2048]{1,0:T(8,128)(2,1)S(1)}, bf16[256,2048]{1,0:T(8,128)(2,1)S(1)}, u32[]{:S(2)}, u32[]{:S(2)}) %collective-permute-start.2) | collective-permute-done | bytes 1048608 | tf_op jit(solution)/shard_map/ppermute | solution.py:36
  139.9 2.5 collective-permute-start.4
  142.4 12.0 %collective-permute-done.3 = bf16[256,2048]{1,0:T(8,128)(2,1)S(1)} collective-permute-done((bf16[256,2048]{1,0:T(8,128)(2,1)S(1)}, bf16[256,2048]{1,0:T(8,128)(2,1)S(1)}, u32[]{:S(2)}, u32[]{:S(2)}) %collective-permute-start.3) | collective-permute-done | bytes 1048608 | tf_op jit(solution)/shard_map/ppermute | solution.py:41
  154.3 10.2 %collective-permute-done.4 = bf16[256,2048]{1,0:T(8,128)(2,1)S(1)} collective-permute-done((bf16[256,2048]{1,0:T(8,128)(2,1)S(1)}, bf16[256,2048]{1,0:T(8,128)(2,1)S(1)}, u32[]{:S(2)}, u32[]{:S(2)}) %collective-permute-start.4) | collective-permute-done | bytes 1048608 | tf_op jit(solution)/shard_map/ppermute | solution.py:36
  164.6 2.5 collective-permute-start.6
  167.0 10.7 %collective-permute-done.5 = bf16[256,2048]{1,0:T(8,128)(2,1)S(1)} collective-permute-done((bf16[256,2048]{1,0:T(8,128)(2,1)S(1)}, bf16[256,2048]{1,0:T(8,128)(2,1)S(1)}, u32[]{:S(2)}, u32[]{:S(2)}) %collective-permute-start.5) | collective-permute-done | bytes 1048608 | tf_op jit(solution)/shard_map/ppermute | solution.py:41
  177.7 11.4 %collective-permute-done.6 = bf16[256,2048]{1,0:T(8,128)(2,1)S(1)} collective-permute-done((bf16[256,2048]{1,0:T(8,128)(2,1)S(1)}, bf16[256,2048]{1,0:T(8,128)(2,1)S(1)}, u32[]{:S(2)}, u32[]{:S(2)}) %collective-permute-start.6) | collective-permute-done | bytes 1048608 | tf_op jit(solution)/shard_map/ppermute | solution.py:36
  189.2 2.5 collective-permute-start.8
  191.7 9.5 %collective-permute-done.7 = bf16[256,2048]{1,0:T(8,128)(2,1)} collective-permute-done((bf16[256,2048]{1,0:T(8,128)(2,1)S(1)}, bf16[256,2048]{1,0:T(8,128)(2,1)}, u32[]{:S(2)}, u32[]{:S(2)}) %collective-permute-start.7) | collective-permute-done | bytes 1048608 | tf_op jit(solution)/shard_map/ppermute | solution.py:41
  201.2 1.3 fusion
  202.5 10.5 %collective-permute-done.8 = bf16[256,2048]{1,0:T(8,128)(2,1)} collective-permute-done((bf16[256,2048]{1,0:T(8,128)(2,1)S(1)}, bf16[256,2048]{1,0:T(8,128)(2,1)}, u32[]{:S(2)}, u32[]{:S(2)}) %collective-permute-start.8) | collective-permute-done | bytes 1048608 | tf_op jit(solution)/shard_map/ppermute | solution.py:36
  213.0 2.6 collective-permute-start.10
  215.6 2.4 constant_dynamic-update-slice_fusion.14
  218.0 2.3 constant_dynamic-update-slice_fusion.13
  220.3 2.3 constant_dynamic-update-slice_fusion.12
  222.6 4.4 %collective-permute-done.9 = bf16[256,2048]{1,0:T(8,128)(2,1)} collective-permute-done((bf16[256,2048]{1,0:T(8,128)(2,1)}, bf16[256,2048]{1,0:T(8,128)(2,1)}, u32[]{:S(2)}, u32[]{:S(2)}) %collective-permute-start.9) | collective-permute-done | bytes 1048608 | tf_op jit(solution)/shard_map/ppermute | solution.py:41
  227.0 2.3 constant_dynamic-update-slice_fusion.11
  229.3 9.7 %collective-permute-done.10 = bf16[256,2048]{1,0:T(8,128)(2,1)} collective-permute-done((bf16[256,2048]{1,0:T(8,128)(2,1)}, bf16[256,2048]{1,0:T(8,128)(2,1)}, u32[]{:S(2)}, u32[]{:S(2)}) %collective-permute-start.10) | collective-permute-done | bytes 1048608 | tf_op jit(solution)/shard_map/ppermute | solution.py:36
  238.9 2.5 collective-permute-start.12
  241.4 1.1 constant_dynamic-update-slice_fusion.10
  242.5 2.3 constant_dynamic-update-slice_fusion.9
  244.9 2.3 constant_dynamic-update-slice_fusion.8
  247.2 2.3 constant_dynamic-update-slice_fusion.7
  249.5 3.1 %collective-permute-done.11 = bf16[256,2048]{1,0:T(8,128)(2,1)S(1)} collective-permute-done((bf16[256,2048]{1,0:T(8,128)(2,1)}, bf16[256,2048]{1,0:T(8,128)(2,1)S(1)}, u32[]{:S(2)}, u32[]{:S(2)}) %collective-permute-start.11) | collective-permute-done | bytes 1048608 | tf_op jit(solution)/shard_map/ppermute | solution.py:41
  252.6 2.4 constant_dynamic-update-slice_fusion.6
  255.0 9.7 %collective-permute-done.12 = bf16[256,2048]{1,0:T(8,128)(2,1)S(1)} collective-permute-done((bf16[256,2048]{1,0:T(8,128)(2,1)}, bf16[256,2048]{1,0:T(8,128)(2,1)S(1)}, u32[]{:S(2)}, u32[]{:S(2)}) %collective-permute-start.12) | collective-permute-done | bytes 1048608 | tf_op jit(solution)/shard_map/ppermute | solution.py:36
  264.7 2.4 collective-permute-start.14
  267.1 2.3 constant_dynamic-update-slice_fusion.5
  269.4 2.3 constant_dynamic-update-slice_fusion.4
  271.7 1.1 constant_dynamic-update-slice_fusion.3
  272.8 1.1 constant_dynamic-update-slice_fusion.2
  273.9 4.2 %collective-permute-done.13 = bf16[256,2048]{1,0:T(8,128)(2,1)S(1)} collective-permute-done((bf16[256,2048]{1,0:T(8,128)(2,1)S(1)}, bf16[256,2048]{1,0:T(8,128)(2,1)S(1)}, u32[]{:S(2)}, u32[]{:S(2)}) %collective-permute-start.13) | collective-permute-done | bytes 1048608 | tf_op jit(solution)/shard_map/ppermute | solution.py:41
  278.1 1.2 constant_dynamic-update-slice_fusion.1
  279.3 1.1 constant_dynamic-update-slice_fusion
  280.4 19.7 %multiply_convert_fusion = bf16[768,2048]{1,0:T(8,128)(2,1)} fusion(bf16[4096,2048]{1,0:T(8,128)(2,1)} %constant_dynamic-update-slice_fusion, bf16[768,4096]{1,0:T(8,128)(2,1)} %param.8, f32[4096]{0:T(1024)S(1)} %copy-done.8, f32[768]{0:T(1024)S(1)} %add_rsqrt_fusion), kind=kOutput, calls=%fused_computation.6 | convolution fusion | flops 12900630528 | bytes 26233856 | tf_op jit(solution)/shard_map/dot_general | solution.py:46
  300.1 1.3 copy.26
  (28 shorter events, 0.1 us)
Async XLA Ops:
  7.2 36.9 %reduce-scatter.2.cloned.1.call-start = ((), (), s32[]{:S(2)}) async-start(), calls=%async_computation.1 | async-start | bytes 3145728 | tf_op jit(solution)/shard_map/reduce_scatter | solution.py:21
  7.9 73.2 %all-gather.2.cloned.1.call-start = ((), (), s32[]{:S(2)}) async-start(), calls=%async_computation.2 | async-start | bytes 3145728 | tf_op jit(solution)/shard_map/all_gather | solution.py:23
  81.1 8.1 %copy-start = (f32[256,2048]{1,0:T(8,128)S(1)}, f32[256,2048]{1,0:T(8,128)}, u32[]{:S(2)}) copy-start(f32[256,2048]{1,0:T(8,128)} %all-gather.2.cloned.1.call-done) | copy-start | bytes 6291460
  81.1 120.1 %copy-start.1 = (bf16[768,4096]{1,0:T(8,128)(2,1)S(1)}, bf16[768,4096]{1,0:T(8,128)(2,1)}, u32[]{:S(2)}) copy-start(bf16[768,4096]{1,0:T(8,128)(2,1)} %param.8) | copy-start | bytes 18874372
  90.4 24.9 %collective-permute-start = (bf16[256,2048]{1,0:T(8,128)(2,1)S(1)}, bf16[256,2048]{1,0:T(8,128)(2,1)S(1)}, u32[]{:S(2)}, u32[]{:S(2)}) collective-permute-start(bf16[256,2048]{1,0:T(8,128)(2,1)S(1)} %get-tuple-element.5), channel_id=1, source_target_pairs={{0,1},{1,2},{2,3},{3,4},{4,5},{5,6},{6,7},{7,8},{8,9},{9,10},{10,1... | collective-permute-start | bytes 3145736 | tf_op jit(solution)/shard_map/ppermute | solution.py:36
  92.3 36.7 %collective-permute-start.1 = (bf16[256,2048]{1,0:T(8,128)(2,1)S(1)}, bf16[256,2048]{1,0:T(8,128)(2,1)S(1)}, u32[]{:S(2)}, u32[]{:S(2)}) collective-permute-start(bf16[256,2048]{1,0:T(8,128)(2,1)S(1)} %get-tuple-element.5), channel_id=1, source_target_pairs={{0,15},{1,0},{2,1},{3,2},{4,3},{5,4},{6,5},{7,6},{8,7},{9,8},{10,9... | collective-permute-start | bytes 3145736 | tf_op jit(solution)/shard_map/ppermute | solution.py:41
  115.3 73.9 %copy-start.2 = (bf16[256,2048]{1,0:T(8,128)(2,1)}, bf16[256,2048]{1,0:T(8,128)(2,1)S(1)}, u32[]{:S(2)}) copy-start(bf16[256,2048]{1,0:T(8,128)(2,1)S(1)} %collective-permute-done) | copy-start | bytes 3145732
  115.3 24.6 %collective-permute-start.2 = (bf16[256,2048]{1,0:T(8,128)(2,1)S(1)}, bf16[256,2048]{1,0:T(8,128)(2,1)S(1)}, u32[]{:S(2)}, u32[]{:S(2)}) collective-permute-start(bf16[256,2048]{1,0:T(8,128)(2,1)S(1)} %collective-permute-done), channel_id=1, source_target_pairs={{0,1},{1,2},{2,3},{3,4},{4,5},{5,6},{6,7},{7,8},{8,9},{9,10},{10,1... | collective-permute-start | bytes 3145736 | tf_op jit(solution)/shard_map/ppermute | solution.py:36
  129.0 13.3 %copy-start.4 = (bf16[256,2048]{1,0:T(8,128)(2,1)}, bf16[256,2048]{1,0:T(8,128)(2,1)S(1)}, u32[]{:S(2)}) copy-start(bf16[256,2048]{1,0:T(8,128)(2,1)S(1)} %collective-permute-done.1) | copy-start | bytes 3145732
  129.0 25.3 %collective-permute-start.3 = (bf16[256,2048]{1,0:T(8,128)(2,1)S(1)}, bf16[256,2048]{1,0:T(8,128)(2,1)S(1)}, u32[]{:S(2)}, u32[]{:S(2)}) collective-permute-start(bf16[256,2048]{1,0:T(8,128)(2,1)S(1)} %collective-permute-done.1), channel_id=1, source_target_pairs={{0,15},{1,0},{2,1},{3,2},{4,3},{5,4},{6,5},{7,6},{8,7},{9,8},{10,9... | collective-permute-start | bytes 3145736 | tf_op jit(solution)/shard_map/ppermute | solution.py:41
  139.9 61.3 %copy-start.7 = (bf16[256,2048]{1,0:T(8,128)(2,1)}, bf16[256,2048]{1,0:T(8,128)(2,1)S(1)}, u32[]{:S(2)}) copy-start(bf16[256,2048]{1,0:T(8,128)(2,1)S(1)} %collective-permute-done.2) | copy-start | bytes 3145732
  139.9 24.7 %collective-permute-start.4 = (bf16[256,2048]{1,0:T(8,128)(2,1)S(1)}, bf16[256,2048]{1,0:T(8,128)(2,1)S(1)}, u32[]{:S(2)}, u32[]{:S(2)}) collective-permute-start(bf16[256,2048]{1,0:T(8,128)(2,1)S(1)} %collective-permute-done.2), channel_id=1, source_target_pairs={{0,1},{1,2},{2,3},{3,4},{4,5},{5,6},{6,7},{7,8},{8,9},{9,10},{10,1... | collective-permute-start | bytes 3145736 | tf_op jit(solution)/shard_map/ppermute | solution.py:36
  154.3 46.9 %copy-start.5 = (bf16[256,2048]{1,0:T(8,128)(2,1)}, bf16[256,2048]{1,0:T(8,128)(2,1)S(1)}, u32[]{:S(2)}) copy-start(bf16[256,2048]{1,0:T(8,128)(2,1)S(1)} %collective-permute-done.3) | copy-start | bytes 3145732
  154.3 23.4 %collective-permute-start.5 = (bf16[256,2048]{1,0:T(8,128)(2,1)S(1)}, bf16[256,2048]{1,0:T(8,128)(2,1)S(1)}, u32[]{:S(2)}, u32[]{:S(2)}) collective-permute-start(bf16[256,2048]{1,0:T(8,128)(2,1)S(1)} %collective-permute-done.3), channel_id=1, source_target_pairs={{0,15},{1,0},{2,1},{3,2},{4,3},{5,4},{6,5},{7,6},{8,7},{9,8},{10,9... | collective-permute-start | bytes 3145736 | tf_op jit(solution)/shard_map/ppermute | solution.py:41
  164.6 24.6 %collective-permute-start.6 = (bf16[256,2048]{1,0:T(8,128)(2,1)S(1)}, bf16[256,2048]{1,0:T(8,128)(2,1)S(1)}, u32[]{:S(2)}, u32[]{:S(2)}) collective-permute-start(bf16[256,2048]{1,0:T(8,128)(2,1)S(1)} %collective-permute-done.4), channel_id=1, source_target_pairs={{0,1},{1,2},{2,3},{3,4},{4,5},{5,6},{6,7},{7,8},{8,9},{9,10},{10,1... | collective-permute-start | bytes 3145736 | tf_op jit(solution)/shard_map/ppermute | solution.py:36
  177.7 13.9 %copy-start.3 = (bf16[256,2048]{1,0:T(8,128)(2,1)}, bf16[256,2048]{1,0:T(8,128)(2,1)S(1)}, u32[]{:S(2)}) copy-start(bf16[256,2048]{1,0:T(8,128)(2,1)S(1)} %collective-permute-done.5) | copy-start | bytes 3145732
  177.7 23.4 %collective-permute-start.7 = (bf16[256,2048]{1,0:T(8,128)(2,1)S(1)}, bf16[256,2048]{1,0:T(8,128)(2,1)}, u32[]{:S(2)}, u32[]{:S(2)}) collective-permute-start(bf16[256,2048]{1,0:T(8,128)(2,1)S(1)} %collective-permute-done.5), channel_id=1, source_target_pairs={{0,15},{1,0},{2,1},{3,2},{4,3},{5,4},{6,5},{7,6},{8,7},{9,8},{10,9... | collective-permute-start | bytes 3145736 | tf_op jit(solution)/shard_map/ppermute | solution.py:41
  189.2 13.3 %copy-start.6 = (bf16[256,2048]{1,0:T(8,128)(2,1)}, bf16[256,2048]{1,0:T(8,128)(2,1)S(1)}, u32[]{:S(2)}) copy-start(bf16[256,2048]{1,0:T(8,128)(2,1)S(1)} %collective-permute-done.6) | copy-start | bytes 3145732
  189.2 23.9 %collective-permute-start.8 = (bf16[256,2048]{1,0:T(8,128)(2,1)S(1)}, bf16[256,2048]{1,0:T(8,128)(2,1)}, u32[]{:S(2)}, u32[]{:S(2)}) collective-permute-start(bf16[256,2048]{1,0:T(8,128)(2,1)S(1)} %collective-permute-done.6), channel_id=1, source_target_pairs={{0,1},{1,2},{2,3},{3,4},{4,5},{5,6},{6,7},{7,8},{8,9},{9,10},{10,1... | collective-permute-start | bytes 3145736 | tf_op jit(solution)/shard_map/ppermute | solution.py:36
  201.2 25.8 %collective-permute-start.9 = (bf16[256,2048]{1,0:T(8,128)(2,1)}, bf16[256,2048]{1,0:T(8,128)(2,1)}, u32[]{:S(2)}, u32[]{:S(2)}) collective-permute-start(bf16[256,2048]{1,0:T(8,128)(2,1)} %collective-permute-done.7), channel_id=1, source_target_pairs={{0,15},{1,0},{2,1},{3,2},{4,3},{5,4},{6,5},{7,6},{8,7},{9,8},{10,9... | collective-permute-start | bytes 3145736 | tf_op jit(solution)/shard_map/ppermute | solution.py:41
  202.5 77.8 %copy-start.8 = (f32[4096]{0:T(1024)S(1)}, f32[4096]{0:T(1024)}, u32[]{:S(2)}) copy-start(f32[4096]{0:T(1024)} %param.9) | copy-start | bytes 49156
  213.0 25.9 %collective-permute-start.10 = (bf16[256,2048]{1,0:T(8,128)(2,1)}, bf16[256,2048]{1,0:T(8,128)(2,1)}, u32[]{:S(2)}, u32[]{:S(2)}) collective-permute-start(bf16[256,2048]{1,0:T(8,128)(2,1)} %collective-permute-done.8), channel_id=1, source_target_pairs={{0,1},{1,2},{2,3},{3,4},{4,5},{5,6},{6,7},{7,8},{8,9},{9,10},{10,1... | collective-permute-start | bytes 3145736 | tf_op jit(solution)/shard_map/ppermute | solution.py:36
  227.0 25.7 %collective-permute-start.11 = (bf16[256,2048]{1,0:T(8,128)(2,1)}, bf16[256,2048]{1,0:T(8,128)(2,1)S(1)}, u32[]{:S(2)}, u32[]{:S(2)}) collective-permute-start(bf16[256,2048]{1,0:T(8,128)(2,1)} %collective-permute-done.9), channel_id=1, source_target_pairs={{0,15},{1,0},{2,1},{3,2},{4,3},{5,4},{6,5},{7,6},{8,7},{9,8},{10,9... | collective-permute-start | bytes 3145736 | tf_op jit(solution)/shard_map/ppermute | solution.py:41
  238.9 25.8 %collective-permute-start.12 = (bf16[256,2048]{1,0:T(8,128)(2,1)}, bf16[256,2048]{1,0:T(8,128)(2,1)S(1)}, u32[]{:S(2)}, u32[]{:S(2)}) collective-permute-start(bf16[256,2048]{1,0:T(8,128)(2,1)} %collective-permute-done.10), channel_id=1, source_target_pairs={{0,1},{1,2},{2,3},{3,4},{4,5},{5,6},{6,7},{7,8},{8,9},{9,10},{10,1... | collective-permute-start | bytes 3145736 | tf_op jit(solution)/shard_map/ppermute | solution.py:36
  252.6 25.5 %collective-permute-start.13 = (bf16[256,2048]{1,0:T(8,128)(2,1)S(1)}, bf16[256,2048]{1,0:T(8,128)(2,1)S(1)}, u32[]{:S(2)}, u32[]{:S(2)}) collective-permute-start(bf16[256,2048]{1,0:T(8,128)(2,1)S(1)} %collective-permute-done.11), channel_id=1, source_target_pairs={{0,15},{1,0},{2,1},{3,2},{4,3},{5,4},{6,5},{7,6},{8,7},{9,8},{10,9... | collective-permute-start | bytes 3145736 | tf_op jit(solution)/shard_map/ppermute | solution.py:41
  264.7 14.6 %collective-permute-start.14 = (bf16[256,2048]{1,0:T(8,128)(2,1)S(1)}, bf16[256,2048]{1,0:T(8,128)(2,1)S(1)}, u32[]{:S(2)}, u32[]{:S(2)}) collective-permute-start(bf16[256,2048]{1,0:T(8,128)(2,1)S(1)} %collective-permute-done.12), channel_id=1, source_target_pairs={{0,1},{1,2},{2,3},{3,4},{4,5},{5,6},{6,7},{7,8},{8,9},{9,10},{10,1... | collective-permute-start | bytes 3145736 | tf_op jit(solution)/shard_map/ppermute | solution.py:36
Sparse Core Ops, SparseCore 0:
  10.2 33.7 reduce-scatter.1
  47.9 33.0 all-gather.1
